TPU v7x, 32 devices: a whole 2x2x4 slice. The times are simulated.
32 devices in a mesh: bank: 4 (over z), zero: 8 (over y, x, core).
Axes of the slice: x: 2, y: 2, z: 4, core: 2. Of those that a mesh axis runs over, the one named last changes fastest.
Arguments:
- train_gate: float32 [64, 2048, 1408], P('bank', 'zero'), may hold values from -0.1875 to 0.1875
- train_up: float32 [64, 2048, 1408], P('bank', 'zero'), may hold values from -0.1875 to 0.1875
- router_weight: float32 [2048, 64], P('zero', 'bank'), may hold values from -0.125 to 0.125
- router_gain: float32 [2048], P('zero'), may hold values from 0.25 to 1.75
Outputs:
- ready_gate: bfloat16 [64, 2048, 1408], P('bank', None, 'zero')
- ready_up: bfloat16 [64, 2048, 1408], P('bank', None, 'zero')
- scale_gate: float32 [64, 1408], P('bank', 'zero')
- scale_up: float32 [64, 1408], P('bank', 'zero')
- serve_router: bfloat16 [2048, 64], replicated
All inputs are finite; a program needn't handle non-finite values. Where the computation divides by a largest or mean magnitude, that divisor is 1e-20 or more.
Results may differ from a plain program's by a relative error of at most 0.012.
Values may be sent and summed in bfloat16 or wider, within the bound.
A program may use at most 192 MiB of HBM per device.

v0:
```python
import jax
import jax.numpy as jnp
from jax import lax
from jax.sharding import PartitionSpec as P

D_MODEL = 2048


def local(train_gate, train_up, router_weight, router_gain):
    total_gate, total_up = (
        lax.psum(jnp.sum(jnp.abs(train_gate), axis=1).astype(jnp.bfloat16), "zero").astype(
            jnp.float32
        ),
        lax.psum(jnp.sum(jnp.abs(train_up), axis=1).astype(jnp.bfloat16), "zero").astype(
            jnp.float32
        ),
    )
    scale_gate = total_gate / D_MODEL
    scale_up = total_up / D_MODEL
    narrow_gate, narrow_up = (
        (train_gate / jnp.expand_dims(scale_gate, 1)).astype(jnp.bfloat16),
        (train_up / jnp.expand_dims(scale_up, 1)).astype(jnp.bfloat16),
    )
    ready_gate, ready_up = (
        lax.all_to_all(narrow_gate, "zero", split_axis=2, concat_axis=1, tiled=True),
        lax.all_to_all(narrow_up, "zero", split_axis=2, concat_axis=1, tiled=True),
    )
    scale_gate = lax.dynamic_slice_in_dim(
        scale_gate, lax.axis_index("zero") * ready_gate.shape[2], ready_gate.shape[2], axis=1
    )
    scale_up = lax.dynamic_slice_in_dim(
        scale_up, lax.axis_index("zero") * ready_up.shape[2], ready_up.shape[2], axis=1
    )
    part_router = (router_weight * router_gain[:, None]).astype(jnp.bfloat16)
    row_router = lax.all_gather(part_router, "zero", axis=0, tiled=True)
    serve_router = lax.all_gather(row_router, "bank", axis=1, tiled=True)
    return (ready_gate, ready_up, scale_gate, scale_up, serve_router)


def solution(mesh):
    in_specs = (P("bank", "zero", None), P("bank", "zero", None), P("zero", "bank"), P("zero"))
    out_specs = (
        P("bank", None, "zero"),
        P("bank", None, "zero"),
        P("bank", "zero"),
        P("bank", "zero"),
        P(),
    )
    return jax.shard_map(local, mesh=mesh, in_specs=in_specs, out_specs=out_specs, check_vma=False)
```

profile of v0, /device:TPU:0, one launch (start us, length us, event | category | flops | bytes accessed | tf_op | source)
XLA Modules:
  0.0 443.6 jit_solution(4854745292164101)
XLA Ops:
  7.2 0.0 all-reduce.3.cloned.1.call-start
  7.2 16.0 %abs_reduce_fusion = (bf16[16,1408]{1,0:T(8,128)(2,1)}, bf16[16,1408]{1,0:T(8,128)(2,1)}) fusion(f32[16,256,1408]{2,1,0:T(8,128)} %param.5, f32[16,256,1408]{2,1,0:T(8,128)} %param.4), kind=kLoop, calls=%fused_computation.1 | loop fusion | flops 23023616 | bytes 46227456 | tf_op jit(solution)/shard_map/reduce_sum | solution.py:14
  23.2 0.0 all-reduce.3.cloned.1.call-update
  23.2 23.7 %copy.22 = f32[16,256,1408]{1,0,2:T(8,128)} copy(f32[16,256,1408]{2,1,0:T(8,128)} %param.5) | data formatting | bytes 46137344 | tf_op args[1]
  46.9 30.6 %all-reduce.3.cloned.1.call-done = (bf16[16,1408]{1,0:T(8,128)(2,1)}, bf16[16,1408]{1,0:T(8,128)(2,1)}) async-done(((bf16[16,1408]{1,0:T(8,128)(2,1)}, bf16[16,1408]{1,0:T(8,128)(2,1)}), (bf16[16,1408]{1,0:T(8,128)(2,1)}, bf16[16,1408]{1,0:T(8,128)(2,1)})) %all-reduce.3.cloned.1.call-update) | async-done | bytes 90128 | tf_op jit(solution)/shard_map/psum | solution.py:11
  77.6 0.8 convert_multiply_fusion
  78.4 0.3 copy.21
  78.7 14.2 %divide_convert_fusion = bf16[16,256,1408]{1,0,2:T(8,128)(2,1)} fusion(f32[16,256,1408]{1,0,2:T(8,128)} %copy.22, f32[16,1408]{0,1:T(8,128)S(1)} %copy.21), kind=kLoop, calls=%fused_computation | loop fusion | flops 11534336 | bytes 34693120 | tf_op jit(solution)/shard_map/convert_element_type | solution.py:22
  92.9 5.2 %all-to-all-start.1 = ((bf16[16,256,1408]{1,0,2:T(8,128)(2,1)}), bf16[16,256,1408]{1,0,2:T(8,128)(2,1)}, u32[]{:S(2)}, u32[]{:S(2)}) async-start(bf16[16,256,1408]{1,0,2:T(8,128)(2,1)} %divide_convert_fusion), calls=%async_computation.1 | async-start | bytes 23068672 | tf_op jit(solution)/shard_map/all_to_all | solution.py:26
  98.1 0.0 copy-start
  98.1 23.7 %copy.18 = f32[16,256,1408]{1,0,2:T(8,128)} copy(f32[16,256,1408]{2,1,0:T(8,128)} %param.4) | data formatting | bytes 46137344 | tf_op args[0]
  121.8 0.0 copy-done
  121.8 0.3 copy.17
  122.1 0.0 copy-start.1
  122.1 0.0 copy-start.2
  122.1 14.2 %divide_convert_fusion.1 = bf16[16,256,1408]{1,0,2:T(8,128)(2,1)} fusion(f32[16,256,1408]{1,0,2:T(8,128)} %copy.18, f32[16,1408]{0,1:T(8,128)S(1)} %copy.17), kind=kLoop, calls=%fused_computation.2 | loop fusion | flops 11534336 | bytes 34693120 | tf_op jit(solution)/shard_map/convert_element_type | solution.py:21
  136.3 89.5 %all-to-all-done.1 = bf16[16,256,1408]{1,0,2:T(8,128)(2,1)} async-done(((bf16[16,256,1408]{1,0,2:T(8,128)(2,1)}), bf16[16,256,1408]{1,0,2:T(8,128)(2,1)}, u32[]{:S(2)}, u32[]{:S(2)}) %all-to-all-start.1) | async-done | bytes 11534368 | tf_op jit(solution)/shard_map/all_to_all | solution.py:26
  225.9 5.3 %all-to-all-start = ((bf16[16,256,1408]{1,0,2:T(8,128)(2,1)}), bf16[16,256,1408]{1,0,2:T(8,128)(2,1)}, u32[]{:S(2)}, u32[]{:S(2)}) async-start(bf16[16,256,1408]{1,0,2:T(8,128)(2,1)} %divide_convert_fusion.1), calls=%async_computation | async-start | bytes 23068672 | tf_op jit(solution)/shard_map/all_to_all | solution.py:25
  231.1 0.0 copy-done.1
  231.2 0.0 copy-done.2
  231.2 130.9 %all_gather.6 = bf16[2048,16]{0,1:T(8,128)(2,1)S(1)} all-gather(bf16[256,16]{0,1:T(8,128)(2,1)S(1)} %multiply_convert_fusion), channel_id=1, replica_groups=mesh['bank'=4,'zero'=8] {'zero'}, dimensions={0}, use_global_device_ids=true | all-gather | bytes 73728 | tf_op jit(solution)/shard_map/all_gather | solution.py:35
  362.1 14.0 %all_gather.7 = bf16[2048,64]{0,1:T(8,128)(2,1)S(1)} all-gather(bf16[2048,16]{0,1:T(8,128)(2,1)S(1)} %all_gather.6), channel_id=1, replica_groups=mesh['bank'=4,'zero'=8] {'bank'}, dimensions={1}, use_global_device_ids=true | all-gather | bytes 327680 | tf_op jit(solution)/shard_map/all_gather | solution.py:36
  376.1 0.7 constant_dynamic-slice_fusion
  376.7 0.7 constant_dynamic-slice_fusion.1
  377.4 11.4 %copy.24 = bf16[16,8,256,176]{2,1,3,0:T(8,128)(2,1)} copy(bf16[16,8,256,176]{2,0,3,1:T(8,128)(2,1)} %bitcast.5) | data formatting | bytes 23068672 | tf_op jit(solution)/shard_map/all_to_all | solution.py:26
  388.8 18.0 %all_to_all.33 = bf16[16,2048,176]{1,2,0:T(8,128)(2,1)} reshape(bf16[16,8,256,176]{2,1,3,0:T(8,128)(2,1)} %copy.24) | data formatting | bytes 23068672 | tf_op jit(solution)/shard_map/all_to_all | solution.py:26
  406.8 0.0 all-to-all-done
  406.8 11.4 %copy.20 = bf16[16,8,256,176]{2,1,3,0:T(8,128)(2,1)} copy(bf16[16,8,256,176]{2,0,3,1:T(8,128)(2,1)} %bitcast.2) | data formatting | bytes 23068672 | tf_op jit(solution)/shard_map/all_to_all | solution.py:25
  418.1 18.0 %all_to_all.29 = bf16[16,2048,176]{1,2,0:T(8,128)(2,1)} reshape(bf16[16,8,256,176]{2,1,3,0:T(8,128)(2,1)} %copy.20) | data formatting | bytes 23068672 | tf_op jit(solution)/shard_map/all_to_all | solution.py:25
  436.1 0.7 copy.30
  (2 shorter events, 0.0 us)
Async XLA Ops:
  7.2 70.4 %all-reduce.3.cloned.1.call-start = ((), (), s32[]{:S(2)}) async-start(), calls=%async_computation.2 | async-start | bytes 180224 | tf_op jit(solution)/shard_map/psum | solution.py:11
  92.9 133.0 %all-to-all-start.1 = ((bf16[16,256,1408]{1,0,2:T(8,128)(2,1)}), bf16[16,256,1408]{1,0,2:T(8,128)(2,1)}, u32[]{:S(2)}, u32[]{:S(2)}) async-start(bf16[16,256,1408]{1,0,2:T(8,128)(2,1)} %divide_convert_fusion), calls=%async_computation.1 | async-start | bytes 23068672 | tf_op jit(solution)/shard_map/all_to_all | solution.py:26
  98.1 23.7 %copy-start = (bf16[16,1408]{1,0:T(8,128)(2,1)S(1)}, bf16[16,1408]{1,0:T(8,128)(2,1)}, u32[]{:S(2)}) copy-start(bf16[16,1408]{1,0:T(8,128)(2,1)} %get-tuple-element.5) | copy-start | bytes 135172
  122.1 109.1 %copy-start.1 = (f32[256,16]{0,1:T(8,128)S(1)}, f32[256,16]{0,1:T(8,128)}, u32[]{:S(2)}) copy-start(f32[256,16]{0,1:T(8,128)} %param.6) | copy-start | bytes 49156
  122.1 109.1 %copy-start.2 = (f32[256]{0:T(256)S(1)}, f32[256]{0:T(256)}, u32[]{:S(2)}) copy-start(f32[256]{0:T(256)} %param.7) | copy-start | bytes 3076
  225.9 180.9 %all-to-all-start = ((bf16[16,256,1408]{1,0,2:T(8,128)(2,1)}), bf16[16,256,1408]{1,0,2:T(8,128)(2,1)}, u32[]{:S(2)}, u32[]{:S(2)}) async-start(bf16[16,256,1408]{1,0,2:T(8,128)(2,1)} %divide_convert_fusion.1), calls=%async_computation | async-start | bytes 23068672 | tf_op jit(solution)/shard_map/all_to_all | solution.py:25
Sparse Core Ops, SparseCore 0:
  23.4 54.1 all-reduce.2
where the time goes:
time: 446 us; the launch traced here: 444 us
  blocking collectives  145 us (33%)
  waiting for transfers between devices  120 us (27%)
  local copies, waits for them, and re-layouts  109 us (24%)
  other arithmetic  45.3 us (10%)
  between operations  14.1 us (3%)
  starting transfers between devices  10.5 us (2%)
    all_gather x1, blocking collectives, local(): row_router = lax.all_gather(part_router, 'zero', axis=0, tiled=True)  131 us
    all_to_all x1, waiting for transfers between devices, local(): lax.all_to_all(narrow_up, 'zero', split_axis=2, concat_axis=1, tiled=True)  89.5 us
    unnamed x9, local copies, waits for them, and re-layouts  48.1 us
    psum x1, waiting for transfers between devices, local(): lax.psum(jnp.sum(jnp.abs(train_gate), axis=1).astype(jnp.bfloat16), 'zero')  30.6 us
    all_to_all x2, local copies, waits for them, and re-layouts, local(): lax.all_to_all(narrow_gate, 'zero', split_axis=2, concat_axis=1, tiled=True)  29.3 us
    all_to_all x2, local copies, waits for them, and re-layouts, local(): lax.all_to_all(narrow_up, 'zero', split_axis=2, concat_axis=1, tiled=True)  29.3 us
    reduce_sum x1, other arithmetic, local(): jnp.sum(jnp.abs(train_up), axis=1).astype(jnp.bfloat16)  16 us
    convert_element_type x1, other arithmetic, local(): (train_up / jnp.expand_dims(scale_up, 1)).astype(jnp.bfloat16)  14.2 us
  transfers between devices with their start and end apart: 3, of which 2 were waited for; matrix products, arithmetic and copies ran while one was open for 17% of the time, Pallas kernels for 0%

commit v1 on v0

--- a/solution.py
+++ b/solution.py
@@ -4,6 +4,12 @@
 from jax.sharding import PartitionSpec as P
 
 D_MODEL = 2048
+
+
+def stacked_exchange(value, axis, split, join):
+    shards = jnp.split(value, lax.axis_size(axis), axis=split)
+    received = lax.all_to_all(jnp.stack(shards), axis, 0, 0)
+    return jnp.concatenate(received, axis=join)
 
 
 def local(train_gate, train_up, router_weight, router_gain):
@@ -22,7 +28,7 @@
         (train_up / jnp.expand_dims(scale_up, 1)).astype(jnp.bfloat16),
     )
     ready_gate, ready_up = (
-        lax.all_to_all(narrow_gate, "zero", split_axis=2, concat_axis=1, tiled=True),
+        stacked_exchange(narrow_gate, "zero", 2, 1),
         lax.all_to_all(narrow_up, "zero", split_axis=2, concat_axis=1, tiled=True),
     )
     scale_gate = lax.dynamic_slice_in_dim(

time: 446 us -> 431 us (0.966)
  local copies, waits for them, and re-layouts: 109 us -> 98.2 us
  other arithmetic: 45.3 us -> 40.8 us
    all_to_all x1, waiting for transfers between devices: 0.01 us -> 89.6 us  [stacked_exchange(): received = lax.all_to_all(jnp.stack(shards), axis, 0, 0)]
    all_to_all x1, waiting for transfers between devices: 89.5 us -> 0.01 us  [local(): lax.all_to_all(narrow_up, 'zero', split_axis=2, concat_axis=1, tiled=True)]
    all_to_all x2 -> x0, local copies, waits for them, and re-layouts: 29.3 us -> none  [local(): lax.all_to_all(narrow_gate, 'zero', split_axis=2, concat_axis=1, tiled=True)]
    reshape x0 -> x1, local copies, waits for them, and re-layouts: none -> 10 us  [stacked_exchange(): return jnp.concatenate(received, axis=join)]
    unnamed x9 -> x16, local copies, waits for them, and re-layouts: 48.1 us -> 56.1 us
where the time goes in v1:
time: 431 us; the launch traced here: 429 us
  blocking collectives  145 us (34%)
  waiting for transfers between devices  121 us (28%)
  local copies, waits for them, and re-layouts  98.2 us (23%)
  other arithmetic  40.8 us (9%)
  between operations  14.1 us (3%)
  starting transfers between devices  10.5 us (2%)
    all_gather x1, blocking collectives, local(): row_router = lax.all_gather(part_router, 'zero', axis=0, tiled=True)  131 us
    all_to_all x1, waiting for transfers between devices, stacked_exchange(): received = lax.all_to_all(jnp.stack(shards), axis, 0, 0)  89.6 us
    unnamed x16, local copies, waits for them, and re-layouts  56.1 us
    psum x1, waiting for transfers between devices, local(): lax.psum(jnp.sum(jnp.abs(train_gate), axis=1).astype(jnp.bfloat16), 'zero')  31 us
    all_to_all x2, local copies, waits for them, and re-layouts, local(): lax.all_to_all(narrow_up, 'zero', split_axis=2, concat_axis=1, tiled=True)  29.3 us
    reduce_sum x1, other arithmetic, local(): jnp.sum(jnp.abs(train_up), axis=1).astype(jnp.bfloat16)  16 us
    convert_element_type x1, other arithmetic, local(): (train_up / jnp.expand_dims(scale_up, 1)).astype(jnp.bfloat16)  14.2 us
    all_gather x1, blocking collectives, local(): serve_router = lax.all_gather(row_router, 'bank', axis=1, tiled=True)  14 us
  transfers between devices with their start and end apart: 3, of which 2 were waited for; matrix products, arithmetic and copies ran while one was open for 17% of the time, Pallas kernels for 0%

profile of v1, /device:TPU:0, one launch (start us, length us, event | category | flops | bytes accessed | tf_op | source)
XLA Modules:
  0.0 429.2 jit_solution(7392823306983214482)
XLA Ops:
  7.2 0.0 all-reduce.3.cloned.1.call-start
  7.2 16.0 %abs_reduce_fusion = (bf16[16,1408]{1,0:T(8,128)(2,1)}, bf16[16,1408]{1,0:T(8,128)(2,1)}) fusion(f32[16,256,1408]{2,1,0:T(8,128)} %param.5, f32[16,256,1408]{2,1,0:T(8,128)} %param.4), kind=kLoop, calls=%fused_computation.1 | loop fusion | flops 23023616 | bytes 46227456 | tf_op jit(solution)/shard_map/reduce_sum | solution.py:20
  23.2 0.0 all-reduce.3.cloned.1.call-update
  23.3 23.3 %copy.21 = f32[16,256,1408]{1,2,0:T(8,128)} copy(f32[16,256,1408]{2,1,0:T(8,128)} %param.4) | data formatting | bytes 46137344 | tf_op args[0]
  46.6 31.0 %all-reduce.3.cloned.1.call-done = (bf16[16,1408]{1,0:T(8,128)(2,1)}, bf16[16,1408]{1,0:T(8,128)(2,1)}) async-done(((bf16[16,1408]{1,0:T(8,128)(2,1)}, bf16[16,1408]{1,0:T(8,128)(2,1)}), (bf16[16,1408]{1,0:T(8,128)(2,1)}, bf16[16,1408]{1,0:T(8,128)(2,1)})) %all-reduce.3.cloned.1.call-update) | async-done | bytes 90128 | tf_op jit(solution)/shard_map/psum | solution.py:17
  77.6 0.8 convert_multiply_fusion.1
  78.4 9.8 %divide_convert_fusion.1 = bf16[16,256,1408]{1,2,0:T(8,128)(2,1)S(1)} fusion(f32[16,256,1408]{1,2,0:T(8,128)} %copy.21, f32[16,1408]{1,0:T(8,128)S(1)} %convert_multiply_fusion.1), kind=kLoop, calls=%fused_computation.2 | loop fusion | flops 11534336 | bytes 34693120 | tf_op jit(solution)/shard_map/convert_element_type | solution.py:27
  88.2 1.2 fusion.7
  89.4 1.2 fusion.6
  90.6 1.2 fusion.5
  91.8 1.2 fusion.4
  93.0 1.2 fusion.3
  94.2 1.2 fusion.2
  95.4 1.2 fusion.1
  96.6 1.2 fusion
  97.8 5.2 %all-to-all-start = ((bf16[8,16,256,176]{2,3,1,0:T(8,128)(2,1)}), bf16[8,16,256,176]{2,3,1,0:T(8,128)(2,1)}, u32[]{:S(2)}, u32[]{:S(2)}) async-start(bf16[8,16,256,176]{2,3,1,0:T(8,128)(2,1)} %fusion), calls=%async_computation | async-start | bytes 23068672 | tf_op jit(solution)/shard_map/all_to_all | solution.py:11
  103.0 0.0 copy-start
  103.0 23.7 %copy.24 = f32[16,256,1408]{1,0,2:T(8,128)} copy(f32[16,256,1408]{2,1,0:T(8,128)} %param.5) | data formatting | bytes 46137344 | tf_op args[1]
  126.7 0.0 copy-done
  126.7 0.3 copy.23
  127.0 14.2 %divide_convert_fusion = bf16[16,256,1408]{1,0,2:T(8,128)(2,1)} fusion(f32[16,256,1408]{1,0,2:T(8,128)} %copy.24, f32[16,1408]{0,1:T(8,128)S(1)} %copy.23), kind=kLoop, calls=%fused_computation | loop fusion | flops 11534336 | bytes 34693120 | tf_op jit(solution)/shard_map/convert_element_type | solution.py:28
  141.2 0.0 copy-start.1
  141.2 0.0 copy-start.2
  141.2 89.6 %all-to-all-done = bf16[8,16,256,176]{2,3,1,0:T(8,128)(2,1)} async-done(((bf16[8,16,256,176]{2,3,1,0:T(8,128)(2,1)}), bf16[8,16,256,176]{2,3,1,0:T(8,128)(2,1)}, u32[]{:S(2)}, u32[]{:S(2)}) %all-to-all-start) | async-done | bytes 11534368 | tf_op jit(solution)/shard_map/all_to_all | solution.py:11
  230.8 5.3 %all-to-all-start.1 = ((bf16[16,256,1408]{1,0,2:T(8,128)(2,1)}), bf16[16,256,1408]{1,0,2:T(8,128)(2,1)}, u32[]{:S(2)}, u32[]{:S(2)}) async-start(bf16[16,256,1408]{1,0,2:T(8,128)(2,1)} %divide_convert_fusion), calls=%async_computation.1 | async-start | bytes 23068672 | tf_op jit(solution)/shard_map/all_to_all | solution.py:32
  236.0 0.0 copy-done.1
  236.0 0.0 copy-done.2
  236.1 130.9 %all_gather.6 = bf16[2048,16]{0,1:T(8,128)(2,1)S(1)} all-gather(bf16[256,16]{0,1:T(8,128)(2,1)S(1)} %multiply_convert_fusion), channel_id=1, replica_groups=mesh['bank'=4,'zero'=8] {'zero'}, dimensions={0}, use_global_device_ids=true | all-gather | bytes 73728 | tf_op jit(solution)/shard_map/all_gather | solution.py:41
  367.0 14.0 %all_gather.7 = bf16[2048,64]{0,1:T(8,128)(2,1)S(1)} all-gather(bf16[2048,16]{0,1:T(8,128)(2,1)S(1)} %all_gather.6), channel_id=1, replica_groups=mesh['bank'=4,'zero'=8] {'bank'}, dimensions={1}, use_global_device_ids=true | all-gather | bytes 327680 | tf_op jit(solution)/shard_map/all_gather | solution.py:42
  381.0 0.7 constant_dynamic-slice_fusion
  381.6 0.7 constant_dynamic-slice_fusion.1
  382.3 10.0 %copy.28 = bf16[8,16,22,8,256]{4,3,0,2,1:T(8,128)(2,1)} copy(bf16[8,16,22,8,256]{4,3,2,1,0:T(8,128)(2,1)} %bitcast.12) | data formatting | bytes 23068672 | tf_op jit(solution)/shard_map/reshape | solution.py:12
  392.3 0.0 all-to-all-done.1
  392.3 11.4 %copy.26 = bf16[16,8,256,176]{2,1,3,0:T(8,128)(2,1)} copy(bf16[16,8,256,176]{2,0,3,1:T(8,128)(2,1)} %bitcast.11) | data formatting | bytes 23068672 | tf_op jit(solution)/shard_map/all_to_all | solution.py:32
  403.7 18.0 %all_to_all.20 = bf16[16,2048,176]{1,2,0:T(8,128)(2,1)} reshape(bf16[16,8,256,176]{2,1,3,0:T(8,128)(2,1)} %copy.26) | data formatting | bytes 23068672 | tf_op jit(solution)/shard_map/all_to_all | solution.py:32
  421.6 0.7 copy.39
  (2 shorter events, 0.0 us)
Async XLA Ops:
  7.2 70.4 %all-reduce.3.cloned.1.call-start = ((), (), s32[]{:S(2)}) async-start(), calls=%async_computation.2 | async-start | bytes 180224 | tf_op jit(solution)/shard_map/psum | solution.py:17
  97.8 133.0 %all-to-all-start = ((bf16[8,16,256,176]{2,3,1,0:T(8,128)(2,1)}), bf16[8,16,256,176]{2,3,1,0:T(8,128)(2,1)}, u32[]{:S(2)}, u32[]{:S(2)}) async-start(bf16[8,16,256,176]{2,3,1,0:T(8,128)(2,1)} %fusion), calls=%async_computation | async-start | bytes 23068672 | tf_op jit(solution)/shard_map/all_to_all | solution.py:11
  103.0 23.7 %copy-start = (bf16[16,1408]{1,0:T(8,128)(2,1)S(1)}, bf16[16,1408]{1,0:T(8,128)(2,1)}, u32[]{:S(2)}) copy-start(bf16[16,1408]{1,0:T(8,128)(2,1)} %get-tuple-element.6) | copy-start | bytes 135172
  141.2 94.9 %copy-start.1 = (f32[256,16]{0,1:T(8,128)S(1)}, f32[256,16]{0,1:T(8,128)}, u32[]{:S(2)}) copy-start(f32[256,16]{0,1:T(8,128)} %param.6) | copy-start | bytes 49156
  141.2 94.9 %copy-start.2 = (f32[256]{0:T(256)S(1)}, f32[256]{0:T(256)}, u32[]{:S(2)}) copy-start(f32[256]{0:T(256)} %param.7) | copy-start | bytes 3076
  230.8 161.6 %all-to-all-start.1 = ((bf16[16,256,1408]{1,0,2:T(8,128)(2,1)}), bf16[16,256,1408]{1,0,2:T(8,128)(2,1)}, u32[]{:S(2)}, u32[]{:S(2)}) async-start(bf16[16,256,1408]{1,0,2:T(8,128)(2,1)} %divide_convert_fusion), calls=%async_computation.1 | async-start | bytes 23068672 | tf_op jit(solution)/shard_map/all_to_all | solution.py:32
Sparse Core Ops, SparseCore 0:
  23.4 54.1 all-reduce.2
